TPU v7x, 32 devices: a whole 2x2x4 slice. The times are simulated.
32 devices in a mesh: row: 8 (over y, x, core), col: 4 (over z).
Axes of the slice: x: 2, y: 2, z: 4, core: 2. Of those that a mesh axis runs over, the one named last changes fastest.
Arguments:
- residual: bfloat16 [8, 4, 2048, 512], P('row', 'col'), may hold values from -6 to 6
- self_tiles: bfloat16 [8, 4, 2048, 2048], P('row', 'col'), may hold values from -0.09375 to 0.09375
- side_tiles: bfloat16 [8, 4, 2048, 2048], P('row', 'col'), may hold values from -0.09375 to 0.09375
- row_cluster_basis: bfloat16 [8, 4, 2048, 32], P('row', 'col'), may hold values from -0.125 to 0.125
- column_cluster_basis: bfloat16 [8, 4, 2048, 32], P('row', 'col'), may hold values from -1 to 1
- couplings: bfloat16 [8, 4, 64, 32, 32], P('row', 'col'), may hold values from -0.1875 to 0.1875
- near_side: int32 [8, 4], P('row', 'col'), may hold values from -1 to 1
- adm_targets: int32 [8, 4, 64], P('row', 'col'), may hold values from 0 to 31, as said below
- adm_ranks: int32 [8, 4, 64], P('row', 'col'), may hold values from 8 to 32
- adm_count: int32 [8, 4], P('row', 'col'), may hold values from 1 to 64
Outputs:
- gradient: float32 [8, 4, 2048, 512], P('row', 'col')
Inputs may be any that keep to these rules, and one draw needn't show every extreme that they name: `near_side`: -1 or +1 names the cluster row before or after around the loop of 8 rows; 0 means no such tile. Each entry of adm_targets for the block row of linear index i is the linear index of a cluster other than i; slot 0 names i - 1 or i + 1, counted round the 32 clusters; targets may repeat.
All inputs are finite; a program needn't handle non-finite values.
Results may differ from a plain program's by a relative error of at most 0.0033.
Values may be sent and summed in bfloat16 or wider, within the bound.
A program may use at most 128 MiB of HBM per device.

v0:
```python
import functools

import jax
import jax.numpy as jnp
from jax import lax
from jax.experimental import pallas as pl
from jax.experimental.pallas import tpu as pltpu
from jax.sharding import PartitionSpec as P

MESH = pl.DeviceIdType.MESH
CORES = 2
MROWS = 256


def contract(a, b):
    return lax.dot_general(
        a, b, (((0,), (0,)), ((), ())), preferred_element_type=jnp.float32
    )


def kernel(
    rows, cols, chunks,
    near_ref, count_ref, tgt_ref, rank_ref, x_hbm, rb_hbm, cb_hbm, coup_hbm, self_hbm, side_hbm,
    out_ref,
    x_ref, rb_ref, cb_ref, coup_ref, self_v, side_v, above, below, acc, table, cbuf, rec,
    tile_sem, out_sem, up_s, up_r, dn_s, dn_r, a_s, a_r, b_s, b_r, c_s, c_r, k_s, k_r,
):
    total = rows * cols
    chips = rows // CORES
    leaf, width = x_ref.shape
    flat, slots = coup_ref.shape
    rank = rb_ref.shape[0]
    row, col = lax.axis_index("row"), lax.axis_index("col")
    core, chip = lax.rem(row, CORES), row // CORES
    me = row * cols + col
    my_slot = (core * cols + col) * chips + chip

    def place(j):
        return (j // cols, lax.rem(j, cols))

    barrier = pltpu.get_barrier_semaphore()

    def greet(k, carry):
        pl.semaphore_signal(
            barrier, inc=1, device_id=place(lax.rem(me + k, total)), device_id_type=MESH
        )
        return carry

    pairs = (
        (rb_hbm, rb_ref), (coup_hbm, coup_ref), (x_hbm, x_ref), (cb_hbm, cb_ref),
        (self_hbm, self_v), (side_hbm, side_v),
    )
    loads = [
        pltpu.make_async_copy(src, dst, tile_sem.at[i]) for i, (src, dst) in enumerate(pairs)
    ]
    for load in loads:
        load.start()
    load_rb, load_coup, load_x, load_cb, load_self, load_side = loads
    lax.fori_loop(1, total, greet, 0)

    load_coup.wait()
    position = lax.broadcasted_iota(jnp.int32, (flat, slots), 0)
    slot = lax.broadcasted_iota(jnp.int32, (flat, slots), 1)
    ranks = rank_ref[...]
    keep = (
        (lax.div(position, rank) < ranks)
        & (lax.rem(position, rank) < ranks)
        & (slot < count_ref[0, 0])
    )
    masked = jnp.where(keep, coup_ref[...].astype(jnp.float32), 0.0).astype(jnp.bfloat16)
    onehot = (lax.broadcasted_iota(jnp.int32, (total, slots), 0) == tgt_ref[...]).astype(
        jnp.float32
    ).astype(jnp.bfloat16)
    sums = lax.dot_general(
        onehot, masked, (((1,), (1,)), ((), ())), preferred_element_type=jnp.float32
    )
    for j in range(total):
        cbuf[j] = sums[j : j + 1, :]
    rec[my_slot] = cbuf[me]
    load_rb.wait()
    load_x.wait()
    table[my_slot] = jnp.dot(
        rb_ref[...], x_ref[...], preferred_element_type=jnp.float32
    ).astype(jnp.bfloat16)

    pl.semaphore_wait(barrier, total - 1)

    def send(src, dst, s, r, to):
        return pltpu.make_async_remote_copy(
            src_ref=src, dst_ref=dst, send_sem=s, recv_sem=r, device_id=to, device_id_type=MESH
        )

    stage_a = []
    for k in range(1, chips):
        other = lax.rem(chip + k, chips)
        copy = send(
            table.at[my_slot], table.at[my_slot], a_s.at[k], a_r.at[k], (other * CORES + core, col)
        )
        copy.start()
        stage_a.append(copy)

    def couple(k):
        j = lax.rem(me + k, total)
        return send(cbuf.at[j], rec.at[my_slot], k_s.at[k], k_r.at[k], place(j))

    def couple_start(k, carry):
        couple(k).start()
        return carry

    lax.fori_loop(1, total, couple_start, 0)

    depth = leaf // chunks
    after, before = lax.rem(row + 1, rows), lax.rem(row + rows - 1, rows)
    ups, downs = [], []
    for c in range(chunks):
        part = pl.ds(c * depth, depth)
        up = send(x_ref.at[part], above.at[part], up_s.at[c], up_r.at[c], (after, col))
        down = send(x_ref.at[part], below.at[part], dn_s.at[c], dn_r.at[c], (before, col))
        up.start()
        down.start()
        ups.append(up)
        downs.append(down)

    tiles = leaf // MROWS

    def own(m, carry):
        at = pl.ds(pl.multiple_of(m * MROWS, MROWS), MROWS)
        acc[at, :] = contract(self_v[:, at], x_ref[...])
        return carry

    load_self.wait()
    lax.fori_loop(0, tiles // 4, own, 0)

    for copy in stage_a:
        copy.wait()
    group = core * cols + col
    stage_b = []
    mine = table.at[pl.ds(group * chips, chips)]
    for k in range(1, cols):
        copy = send(mine, mine, b_s.at[k], b_r.at[k], (row, lax.rem(col + k, cols)))
        copy.start()
        stage_b.append(copy)
    lax.fori_loop(tiles // 4, tiles, own, 0)

    for copy in stage_b:
        copy.wait()
    half = table.at[pl.ds(core * (cols * chips), cols * chips)]
    stage_c = send(half, half, c_s, c_r, (chip * CORES + (1 - core), col))
    stage_c.start()

    side = near_ref[0, 0]
    from_above = jnp.where(side == -1, 1.0, 0.0).astype(jnp.float32)
    from_below = jnp.where(side == 1, 1.0, 0.0).astype(jnp.float32)
    load_side.wait()

    def near(c, finish):
        ups[c].wait()
        downs[c].wait()
        part = pl.ds(c * depth, depth)
        values = (
            above[part, :].astype(jnp.float32) * from_above
            + below[part, :].astype(jnp.float32) * from_below
        ).astype(jnp.bfloat16)

        def body(m, carry):
            at = pl.ds(pl.multiple_of(m * MROWS, MROWS), MROWS)
            acc[at, :] += contract(side_v[part, at], values)
            if finish:
                pltpu.make_async_copy(acc.at[at], out_ref.at[at], out_sem.at[m]).start()
            return carry

        lax.fori_loop(0, tiles, body, 0)

    near(0, False)
    near(1, False)
    stage_c.wait()

    def couple_wait(k, carry):
        couple(k).wait()
        return carry

    lax.fori_loop(1, total, couple_wait, 0)
    batch = 8
    diagonal = (
        lax.div(lax.broadcasted_iota(jnp.int32, (rank, flat), 1), rank)
        == lax.broadcasted_iota(jnp.int32, (rank, flat), 0)
    )
    fold = (
        lax.rem(lax.broadcasted_iota(jnp.int32, (flat, rank), 0), rank)
        == lax.broadcasted_iota(jnp.int32, (flat, rank), 1)
    ).astype(jnp.float32).astype(jnp.bfloat16)

    def gather(g, dual):
        spread = [
            jnp.where(diagonal, rec[g * batch + s], 0.0).astype(jnp.bfloat16) for s in range(batch)
        ]
        blocks = jnp.dot(
            jnp.concatenate(spread, axis=0), fold, preferred_element_type=jnp.float32
        ).astype(jnp.bfloat16)
        coefs = table[pl.ds(g * batch, batch)].reshape(batch * rank, width)
        return dual + contract(blocks, coefs)

    dual = lax.fori_loop(0, total // batch, gather, jnp.zeros((rank, width), jnp.float32))
    dual = dual.astype(jnp.bfloat16)

    def distant(m, carry):
        at = pl.ds(pl.multiple_of(m * MROWS, MROWS), MROWS)
        acc[at, :] += contract(cb_ref[:, at], dual)
        return carry

    load_cb.wait()
    lax.fori_loop(0, tiles, distant, 0)
    for c in range(2, chunks):
        near(c, c == chunks - 1)

    def drain(m, carry):
        at = pl.ds(pl.multiple_of(m * MROWS, MROWS), MROWS)
        pltpu.make_async_copy(acc.at[at], out_ref.at[at], out_sem.at[m]).wait()
        return carry

    lax.fori_loop(0, tiles, drain, 0)


def on_device(
    rows, cols, residual, self_tiles, side_tiles, row_cluster_basis, column_cluster_basis,
    couplings, near_side, adm_targets, adm_ranks, adm_count,
):
    leaf, width = residual.shape[2:]
    slots, rank = couplings.shape[2:4]
    total, chips, chunks = rows * cols, rows // CORES, 8
    vmem = pl.BlockSpec(memory_space=pltpu.VMEM)
    smem = pl.BlockSpec(memory_space=pltpu.SMEM)
    anywhere = pl.BlockSpec(memory_space=pl.ANY)
    dma = pltpu.SemaphoreType.DMA
    gradient = pl.pallas_call(
        functools.partial(kernel, rows, cols, chunks),
        out_shape=jax.ShapeDtypeStruct((leaf, width), jnp.float32),
        in_specs=[smem, smem, vmem, vmem] + [anywhere] * 6,
        out_specs=anywhere,
        scratch_shapes=[
            pltpu.VMEM((leaf, width), jnp.bfloat16),
            pltpu.VMEM((rank, leaf), jnp.bfloat16),
            pltpu.VMEM((rank, leaf), jnp.bfloat16),
            pltpu.VMEM((rank * rank, slots), jnp.bfloat16),
            pltpu.VMEM((leaf, leaf), jnp.bfloat16),
            pltpu.VMEM((leaf, leaf), jnp.bfloat16),
            pltpu.VMEM((leaf, width), jnp.bfloat16),
            pltpu.VMEM((leaf, width), jnp.bfloat16),
            pltpu.VMEM((leaf, width), jnp.float32),
            pltpu.VMEM((total, rank, width), jnp.bfloat16),
            pltpu.VMEM((total, 1, rank * rank), jnp.float32),
            pltpu.VMEM((total, 1, rank * rank), jnp.float32),
            dma((6,)), dma((leaf // MROWS,)),
            dma((chunks,)), dma((chunks,)), dma((chunks,)), dma((chunks,)),
            dma((chips,)), dma((chips,)), dma((cols,)), dma((cols,)), dma, dma,
            dma((total,)), dma((total,)),
        ],
        compiler_params=pltpu.CompilerParams(
            collective_id=0, has_side_effects=True, vmem_limit_bytes=60 * 1024 * 1024
        ),
    )(
        near_side, adm_count, adm_targets.reshape(1, slots), adm_ranks.reshape(1, slots),
        residual[0, 0], row_cluster_basis[0, 0].T, column_cluster_basis[0, 0].T,
        couplings.reshape(slots, rank * rank).T, self_tiles[0, 0], side_tiles[0, 0],
    )
    return gradient[None, None]


def solution(mesh):
    placed = (
        P("row", "col", None, None),
        P("row", "col", None, None),
        P("row", "col", None, None),
        P("row", "col", None, None),
        P("row", "col", None, None),
        P("row", "col", None, None, None),
        P("row", "col"),
        P("row", "col", None),
        P("row", "col", None),
        P("row", "col"),
    )
    return jax.shard_map(
        functools.partial(on_device, mesh.shape["row"], mesh.shape["col"]),
        mesh=mesh,
        in_specs=placed,
        out_specs=P("row", "col", None, None),
        check_vma=False,
    )
```

profile of v0, /device:TPU:0, one launch (start us, length us, event | category | flops | bytes accessed | tf_op | source)
XLA Modules:
  0.0 67.0 jit_solution(5637327454909040840)
XLA Ops:
  1.3 61.0 %shard_map.100 = f32[2048,512]{1,0:T(8,128)} custom-call(s32[1,1]{1,0:T(1,128)S(6)} %copy.12.near_ref, s32[1,1]{1,0:T(1,128)S(6)} %copy.13.count_ref, s32[1,64]{1,0:T(1,128)} %bitcast.22, s32[1,64]{1,0:T(1,128)} %bitcast.23, bf16[2048,512]{1,0:T(8,128)(2,1)} %bitcast.18, bf16[32,2048]{1,0:T(8,128)(2,1)} %bitcast.20, bf16[32,2048]{1,0:T(8,128)(2,1)} %bitcast.21, ...), custom_call_target="tpu_custom_call" | custom-call | tf_op jit(solution)/shard_map/pallas_call | solution.py:235
  62.3 4.6 %copy.14 = f32[1,1,2048,512]{3,2,1,0:T(8,128)} copy(f32[1,1,2048,512]{3,2,1,0:T(8,128)} %bitcast.15) | data formatting | bytes 8388608
where the time goes:
time: 67.2 us; the launch traced here: 67 us
  Pallas kernels  61 us (91%)
  local copies, waits for them, and re-layouts  4.64 us (7%)
  between operations  1.3 us (2%)
    pallas_call x1, Pallas kernels, on_device(): pl.pallas_call(functools.partial(kernel, rows, cols, chunks), out_shape=j...  61 us
    unnamed x1, local copies, waits for them, and re-layouts  4.64 us

commit v1 on v0

v1 whole, which is shorter than its diff:
```python
import functools

import jax
import jax.numpy as jnp
from jax import lax
from jax.experimental import pallas as pl
from jax.experimental.pallas import tpu as pltpu
from jax.sharding import PartitionSpec as P

MESH = pl.DeviceIdType.MESH
CORES = 2
LANES = 128
TILE = 256
NEAR_TILE = 512
FIRST = 3


def contract(a, b):
    return lax.dot_general(
        a, b, (((0,), (0,)), ((), ())), preferred_element_type=jnp.float32
    )


def pieces_of(leaf, blocks):
    quarter = leaf // 4
    pieces = [(c, r * quarter, quarter) for c in range(blocks) for r in range(4)]
    c, start, size = pieces.pop()
    return pieces + [(c, start, size // 2), (c, start + size // 2, size // 2)]


def kernel(
    rows, cols, pieces,
    near_hbm, count_hbm, tgt_hbm, rank_hbm, x_hbm, rb_hbm, cb_hbm, coup_hbm, self_hbm, side_hbm,
    out_ref,
    near_ref, count_ref, tgt_ref, rank_ref, xf, xc, rb_ref, cb_ref, coup_ref, self_v, side_v,
    above, below, table, flat, mbuf, dpart, dcore, mout, min_ref,
    load_sem, xc_sem, up_s, up_r, dn_s, dn_r, c_s, c_r, m_s, m_r, d_s, d_r, e_s, e_r,
):
    half_chips = rows // CORES // 2
    groups = cols * half_chips
    leaf, width = xf.shape
    blocks = width // LANES
    rank = rb_ref.shape[0]
    positions, slots = coup_ref.shape
    row, col = lax.axis_index("row"), lax.axis_index("col")
    core, chip = lax.rem(row, CORES), row // CORES
    mirror, pair = lax.rem(chip, 2), chip // 2
    group = col * half_chips + pair

    def at_group(g):
        return (((lax.rem(g, half_chips)) * 2 + mirror) * CORES + core, g // half_chips)

    after = (lax.rem(row + 1, rows), col)
    before = (lax.rem(row + rows - 1, rows), col)
    partner = (chip * CORES + (1 - core), col)
    opposite = ((pair * 2 + (1 - mirror)) * CORES + core, col)
    strides = []
    while groups >> (len(strides) + 1):
        strides.append(groups >> (len(strides) + 1))
    others = [at_group(group + h * (1 - 2 * lax.rem(group // h, 2))) for h in strides]

    loads = [
        pltpu.make_async_copy(
            x_hbm.at[:, pl.ds(c * LANES, LANES)], xc.at[c], xc_sem.at[c]
        )
        for c in range(blocks)
    ]
    names = (
        (rb_hbm, rb_ref), (x_hbm, xf), (coup_hbm, coup_ref), (tgt_hbm, tgt_ref),
        (rank_hbm, rank_ref), (count_hbm, count_ref), (near_hbm, near_ref),
        (self_hbm, self_v), (cb_hbm, cb_ref), (side_hbm, side_v),
    )
    rest = [
        pltpu.make_async_copy(src, dst, load_sem.at[i]) for i, (src, dst) in enumerate(names)
    ]
    for load in loads + rest:
        load.start()
    (
        load_rb, load_x, load_coup, load_tgt, load_rank, load_count, load_near,
        load_self, load_cb, load_side,
    ) = rest

    barrier = pltpu.get_barrier_semaphore()
    friends = [after, before, opposite] + others
    for friend in friends:
        pl.semaphore_signal(barrier, inc=1, device_id=friend, device_id_type=MESH)

    load_rb.wait()
    load_x.wait()
    table[0] = jnp.dot(rb_ref[...], xf[...], preferred_element_type=jnp.float32).astype(
        jnp.bfloat16
    )
    for load in loads:
        load.wait()

    pl.semaphore_wait(barrier, len(friends))

    def send(src, dst, s, r, to):
        return pltpu.make_async_remote_copy(
            src_ref=src, dst_ref=dst, send_sem=s, recv_sem=r, device_id=to, device_id_type=MESH
        )

    hops = []
    for i, (c, start, size) in enumerate(pieces):
        part = pl.ds(start, size)
        hops.append((
            send(xc.at[c, part], above.at[c, part], up_s.at[i], up_r.at[i], after),
            send(xc.at[c, part], below.at[c, part], dn_s.at[i], dn_r.at[i], before),
        ))

    def launch(some):
        for up, down in some:
            up.start()
            down.start()

    early = sum(1 for c, _, _ in pieces if c < FIRST)
    launch(hops[:early])

    for load in (load_coup, load_tgt, load_rank, load_count):
        load.wait()
    position = lax.broadcasted_iota(jnp.int32, (positions, slots), 0)
    slot = lax.broadcasted_iota(jnp.int32, (positions, slots), 1)
    ranks = rank_ref[...]
    keep = (
        (lax.div(position, rank) < ranks)
        & (lax.rem(position, rank) < ranks)
        & (slot < count_ref[...])
    )
    masked = jnp.where(keep, coup_ref[...].astype(jnp.float32), 0.0).astype(jnp.bfloat16)
    index = lax.broadcasted_iota(jnp.int32, (4 * groups, slots), 0)
    kind, member = lax.div(index, groups), lax.rem(index, groups)
    target = (
        (lax.rem(member, half_chips) * 2 + lax.rem(kind, 2)) * CORES + lax.div(kind, 2)
    ) * cols + lax.div(member, half_chips)
    onehot = (target == tgt_ref[...]).astype(jnp.float32).astype(jnp.bfloat16)
    sums = lax.dot_general(
        onehot, masked, (((1,), (1,)), ((), ())), preferred_element_type=jnp.float32
    )
    per = LANES // rank
    place = lax.broadcasted_iota(jnp.int32, (groups, LANES), 1) // rank
    for a in range(rank):
        base = a // per * LANES
        line = jnp.zeros((groups, LANES), jnp.float32)
        for q in range(4):
            value = sums[q * groups : (q + 1) * groups, base : base + LANES]
            shift = (q - a % per) % per * rank
            if shift:
                value = pltpu.roll(value, shift, 1)
            line = jnp.where(place == q, value, line)
        flat[a] = line
    for g in range(groups):
        mbuf[0, g] = flat[:, g, :].astype(jnp.bfloat16)

    tiles = leaf // TILE

    def own(m, carry):
        at = pl.ds(pl.multiple_of(m * TILE, TILE), TILE)
        out_ref[at, :] = contract(self_v[:, at], xf[...])
        return carry

    load_self.wait()
    steps = len(strides) + 1
    done = 0
    lax.fori_loop(0, 1, own, 0)
    done = 1
    for k, h in enumerate(strides):
        n = 1 << k
        theirs = group // (2 * h) * (2 * h) + (1 - lax.rem(group // h, 2)) * h
        coefs = send(
            table.at[pl.ds(0, n)], table.at[pl.ds(n, n)], c_s.at[k], c_r.at[k], others[k]
        )
        blocks_out = mbuf.at[pl.ds(0, n), pl.ds(theirs, h)]
        blocks_in = mbuf.at[pl.ds(n, n), pl.ds(theirs, h)]
        coupled = send(blocks_out, blocks_in, m_s.at[k], m_r.at[k], others[k])
        coefs.start()
        coupled.start()
        upto = 1 + (tiles - 1) * (k + 1) // steps
        lax.fori_loop(done, upto, own, 0)
        done = upto
        coefs.wait()
        coupled.wait()

    part = contract(
        mbuf[:, group].reshape(groups * rank, LANES), table[...].reshape(groups * rank, width)
    )
    dpart[...] = part.reshape(4, rank, width)
    lax.fori_loop(done, tiles, own, 0)
    swap = send(dpart.at[pl.ds(2 * (1 - core), 2)], dcore, d_s, d_r, partner)
    swap.start()
    load_near.wait()
    load_side.wait()
    from_above = jnp.where(near_ref[...] == -1, 1.0, 0.0).astype(jnp.float32)
    from_below = jnp.where(near_ref[...] == 1, 1.0, 0.0).astype(jnp.float32)

    def near(c, some):
        for i in some:
            hops[i][0].wait()
            hops[i][1].wait()
        start = pieces[some[0]][1]
        size = sum(pieces[i][2] for i in some)
        part = pl.ds(start, size)
        values = (
            above[c, part, :].astype(jnp.float32) * from_above
            + below[c, part, :].astype(jnp.float32) * from_below
        ).astype(jnp.bfloat16)
        lanes = pl.ds(c * LANES, LANES)

        def body(m, carry):
            at = pl.ds(pl.multiple_of(m * NEAR_TILE, NEAR_TILE), NEAR_TILE)
            out_ref[at, lanes] += contract(side_v[part, at], values)
            return carry

        lax.fori_loop(0, leaf // NEAR_TILE, body, 0)

    def members(c):
        return [i for i, p in enumerate(pieces) if p[0] == c]

    swap.wait()
    mout[...] = (dpart[2 * core + 1 - mirror] + dcore[1 - mirror]).astype(jnp.bfloat16)
    cross = send(mout, min_ref, e_s, e_r, opposite)
    cross.start()
    launch(hops[early:])
    for c in range(FIRST - 1):
        near(c, members(c))
    cross.wait()
    dual = (
        dpart[2 * core + mirror] + dcore[mirror] + min_ref[...].astype(jnp.float32)
    ).astype(jnp.bfloat16)

    def distant(m, carry):
        at = pl.ds(pl.multiple_of(m * TILE, TILE), TILE)
        out_ref[at, :] += contract(cb_ref[:, at], dual)
        return carry

    load_cb.wait()
    lax.fori_loop(0, tiles, distant, 0)
    for c in range(FIRST - 1, blocks - 1):
        near(c, members(c))
    for i in members(blocks - 1):
        near(blocks - 1, [i])


def on_device(
    rows, cols, residual, self_tiles, side_tiles, row_cluster_basis, column_cluster_basis,
    couplings, near_side, adm_targets, adm_ranks, adm_count,
):
    leaf, width = residual.shape[2:]
    slots, rank = couplings.shape[2:4]
    groups = cols * (rows // CORES // 2)
    blocks = width // LANES
    pieces = pieces_of(leaf, blocks)
    stages = groups.bit_length() - 1
    count = len(pieces)
    hbm = pl.BlockSpec(memory_space=pltpu.HBM)
    dma = pltpu.SemaphoreType.DMA
    bf16 = jnp.bfloat16
    gradient = pl.pallas_call(
        functools.partial(kernel, rows, cols, pieces),
        out_shape=pltpu.VMEM((leaf, width), jnp.float32),
        in_specs=[hbm] * 10,
        out_specs=pl.BlockSpec(memory_space=pltpu.VMEM),
        scratch_shapes=[
            pltpu.VMEM((1, 1), jnp.int32),
            pltpu.VMEM((1, 1), jnp.int32),
            pltpu.VMEM((1, slots), jnp.int32),
            pltpu.VMEM((1, slots), jnp.int32),
            pltpu.VMEM((leaf, width), bf16),
            pltpu.VMEM((blocks, leaf, LANES), bf16),
            pltpu.VMEM((rank, leaf), bf16),
            pltpu.VMEM((rank, leaf), bf16),
            pltpu.VMEM((rank * rank, slots), bf16),
            pltpu.VMEM((leaf, leaf), bf16),
            pltpu.VMEM((leaf, leaf), bf16),
            pltpu.VMEM((blocks, leaf, LANES), bf16),
            pltpu.VMEM((blocks, leaf, LANES), bf16),
            pltpu.VMEM((groups, rank, width), bf16),
            pltpu.VMEM((rank, groups, LANES), jnp.float32),
            pltpu.VMEM((groups, groups, rank, LANES), bf16),
            pltpu.VMEM((4, rank, width), jnp.float32),
            pltpu.VMEM((2, rank, width), jnp.float32),
            pltpu.VMEM((rank, width), bf16),
            pltpu.VMEM((rank, width), bf16),
            dma((10,)), dma((blocks,)),
            dma((count,)), dma((count,)), dma((count,)), dma((count,)),
            dma((stages,)), dma((stages,)), dma((stages,)), dma((stages,)),
            dma, dma, dma, dma,
        ],
        compiler_params=pltpu.CompilerParams(
            collective_id=0, has_side_effects=True, vmem_limit_bytes=58 * 1024 * 1024
        ),
    )(
        near_side, adm_count, adm_targets.reshape(1, slots), adm_ranks.reshape(1, slots),
        residual[0, 0], row_cluster_basis[0, 0].T, column_cluster_basis[0, 0].T,
        couplings.reshape(slots, rank * rank).T, self_tiles[0, 0], side_tiles[0, 0],
    )
    return gradient[None, None]


def solution(mesh):
    placed = (
        P("row", "col", None, None),
        P("row", "col", None, None),
        P("row", "col", None, None),
        P("row", "col", None, None),
        P("row", "col", None, None),
        P("row", "col", None, None, None),
        P("row", "col"),
        P("row", "col", None),
        P("row", "col", None),
        P("row", "col"),
    )
    return jax.shard_map(
        functools.partial(on_device, mesh.shape["row"], mesh.shape["col"]),
        mesh=mesh,
        in_specs=placed,
        out_specs=P("row", "col", None, None),
        check_vma=False,
    )
```

time: 67.2 us -> 58.8 us (0.87)
  Pallas kernels: 61 us -> 55.4 us
  local copies, waits for them, and re-layouts: 4.64 us -> 2.02 us
    pallas_call x1, Pallas kernels: 61 us -> 55.4 us  [on_device(): pl.pallas_call(functools.partial(kernel, rows, cols, pieces), out_shape=p...]
    unnamed x1, local copies, waits for them, and re-layouts: 4.64 us -> 2.02 us
where the time goes in v1:
time: 58.8 us; the launch traced here: 58.7 us
  Pallas kernels  55.4 us (94%)
  local copies, waits for them, and re-layouts  2.02 us (3%)
  between operations  1.3 us (2%)
    pallas_call x1, Pallas kernels, on_device(): pl.pallas_call(functools.partial(kernel, rows, cols, pieces), out_shape=p...  55.4 us
    unnamed x1, local copies, waits for them, and re-layouts  2.02 us

profile of v1, /device:TPU:0, one launch (start us, length us, event | category | flops | bytes accessed | tf_op | source)
XLA Modules:
  0.0 58.7 jit_solution(1067917910956962951)
XLA Ops:
  1.3 55.4 %shard_map.100 = f32[2048,512]{1,0:T(8,128)S(1)} custom-call(s32[1,1]{1,0:T(1,128)S(6)} %copy.13.near_hbm, s32[1,1]{1,0:T(1,128)S(6)} %copy.14.count_hbm, s32[1,64]{1,0:T(1,128)} %bitcast.22, s32[1,64]{1,0:T(1,128)} %bitcast.23, bf16[2048,512]{1,0:T(8,128)(2,1)} %bitcast.18, bf16[32,2048]{1,0:T(8,128)(2,1)} %bitcast.20, bf16[32,2048]{1,0:T(8,128)(2,1)} %bitcast.21, ...), custom_call_target="tpu_custom_call" | custom-call | tf_op jit(solution)/shard_map/pallas_call | solution.py:257
  56.7 2.0 %copy.12 = f32[1,1,2048,512]{3,2,1,0:T(8,128)} copy(f32[1,1,2048,512]{3,2,1,0:T(8,128)S(1)} %bitcast.15) | data formatting | bytes 8388608

commit v2 on v1

--- a/solution.py
+++ b/solution.py
@@ -12,7 +12,7 @@
 LANES = 128
 TILE = 256
 NEAR_TILE = 512
-FIRST = 3
+EARLY = 10
 
 
 def contract(a, b):
@@ -33,8 +33,8 @@
     near_hbm, count_hbm, tgt_hbm, rank_hbm, x_hbm, rb_hbm, cb_hbm, coup_hbm, self_hbm, side_hbm,
     out_ref,
     near_ref, count_ref, tgt_ref, rank_ref, xf, xc, rb_ref, cb_ref, coup_ref, self_v, side_v,
-    above, below, table, flat, mbuf, dpart, dcore, mout, min_ref,
-    load_sem, xc_sem, up_s, up_r, dn_s, dn_r, c_s, c_r, m_s, m_r, d_s, d_r, e_s, e_r,
+    above, below, turned, table, flat, mbuf, dpart, dcore, mout, min_ref,
+    load_sem, xc_sem, up_s, up_r, dn_s, dn_r, c_s, c_r, m_s, m_r, d_s, d_r, e_s, e_r, relay,
 ):
     half_chips = rows // CORES // 2
     groups = cols * half_chips
@@ -59,6 +59,21 @@
         strides.append(groups >> (len(strides) + 1))
     others = [at_group(group + h * (1 - 2 * lax.rem(group // h, 2))) for h in strides]
 
+    relayed = cols % 4 == 0
+    quad = lax.rem(col, 4)
+    middle = lax.rem((quad + 1) // 2, 2)
+    between = (row, col + 3 - 2 * quad)
+    friends = [after, before, opposite]
+    friends += [d for d, h in zip(others, strides) if not (relayed and h == 2 * half_chips)]
+    barrier = pltpu.get_barrier_semaphore()
+    for friend in friends:
+        pl.semaphore_signal(barrier, inc=1, device_id=friend, device_id_type=MESH)
+    if relayed:
+
+        @pl.when(middle == 1)
+        def _():
+            pl.semaphore_signal(barrier, inc=1, device_id=between, device_id_type=MESH)
+
     loads = [
         pltpu.make_async_copy(
             x_hbm.at[:, pl.ds(c * LANES, LANES)], xc.at[c], xc_sem.at[c]
@@ -80,11 +95,6 @@
         load_self, load_cb, load_side,
     ) = rest
 
-    barrier = pltpu.get_barrier_semaphore()
-    friends = [after, before, opposite] + others
-    for friend in friends:
-        pl.semaphore_signal(barrier, inc=1, device_id=friend, device_id_type=MESH)
-
     load_rb.wait()
     load_x.wait()
     table[0] = jnp.dot(rb_ref[...], xf[...], preferred_element_type=jnp.float32).astype(
@@ -93,7 +103,7 @@
     for load in loads:
         load.wait()
 
-    pl.semaphore_wait(barrier, len(friends))
+    pl.semaphore_wait(barrier, len(friends) + middle if relayed else len(friends))
 
     def send(src, dst, s, r, to):
         return pltpu.make_async_remote_copy(
@@ -113,8 +123,14 @@
             up.start()
             down.start()
 
-    early = sum(1 for c, _, _ in pieces if c < FIRST)
-    launch(hops[:early])
+    launch(hops[:EARLY])
+    if relayed:
+
+        @pl.when(middle == 1)
+        def _():
+            for to in (col - 1, col + 1):
+                pl.semaphore_signal(relay, inc=1, device_id=(row, to), device_id_type=MESH)
+
 
     for load in (load_coup, load_tgt, load_rank, load_count):
         load.wait()
@@ -172,6 +188,8 @@
         blocks_out = mbuf.at[pl.ds(0, n), pl.ds(theirs, h)]
         blocks_in = mbuf.at[pl.ds(n, n), pl.ds(theirs, h)]
         coupled = send(blocks_out, blocks_in, m_s.at[k], m_r.at[k], others[k])
+        if relayed and h == 2 * half_chips:
+            pl.semaphore_wait(relay, 1)
         coefs.start()
         coupled.start()
         upto = 1 + (tiles - 1) * (k + 1) // steps
@@ -192,18 +210,19 @@
     from_above = jnp.where(near_ref[...] == -1, 1.0, 0.0).astype(jnp.float32)
     from_below = jnp.where(near_ref[...] == 1, 1.0, 0.0).astype(jnp.float32)
 
-    def near(c, some):
+    def neighbour(c, some):
         for i in some:
             hops[i][0].wait()
             hops[i][1].wait()
-        start = pieces[some[0]][1]
-        size = sum(pieces[i][2] for i in some)
-        part = pl.ds(start, size)
+        part = pl.ds(pieces[some[0]][1], sum(pieces[i][2] for i in some))
         values = (
             above[c, part, :].astype(jnp.float32) * from_above
             + below[c, part, :].astype(jnp.float32) * from_below
         ).astype(jnp.bfloat16)
-        lanes = pl.ds(c * LANES, LANES)
+        return part, values, pl.ds(c * LANES, LANES)
+
+    def near(c, some):
+        part, values, lanes = neighbour(c, some)
 
         def body(m, carry):
             at = pl.ds(pl.multiple_of(m * NEAR_TILE, NEAR_TILE), NEAR_TILE)
@@ -219,8 +238,8 @@
     mout[...] = (dpart[2 * core + 1 - mirror] + dcore[1 - mirror]).astype(jnp.bfloat16)
     cross = send(mout, min_ref, e_s, e_r, opposite)
     cross.start()
-    launch(hops[early:])
-    for c in range(FIRST - 1):
+    launch(hops[EARLY:])
+    for c in range(blocks - 2):
         near(c, members(c))
     cross.wait()
     dual = (
@@ -234,10 +253,25 @@
 
     load_cb.wait()
     lax.fori_loop(0, tiles, distant, 0)
-    for c in range(FIRST - 1, blocks - 1):
+    for c in range(blocks - 2, blocks - 1):
         near(c, members(c))
-    for i in members(blocks - 1):
+    last = len(pieces) - 1
+    final = pl.ds(pieces[last][1], pieces[last][2])
+
+    def turn(m, carry):
+        at = pl.ds(pl.multiple_of(m * TILE, TILE), TILE)
+        turned[at, :] = side_v[final, at].T
+        return carry
+
+    lax.fori_loop(0, tiles, turn, 0)
+    for i in members(blocks - 1)[:-1]:
         near(blocks - 1, [i])
+    _, values, lanes = neighbour(blocks - 1, [last])
+    for m in range(leaf // NEAR_TILE):
+        at = pl.ds(m * NEAR_TILE, NEAR_TILE)
+        out_ref[at, lanes] += jnp.dot(
+            turned[at, :], values, preferred_element_type=jnp.float32
+        )
 
 
 def on_device(
@@ -273,6 +307,7 @@
             pltpu.VMEM((leaf, leaf), bf16),
             pltpu.VMEM((blocks, leaf, LANES), bf16),
             pltpu.VMEM((blocks, leaf, LANES), bf16),
+            pltpu.VMEM((leaf, pieces[-1][2]), bf16),
             pltpu.VMEM((groups, rank, width), bf16),
             pltpu.VMEM((rank, groups, LANES), jnp.float32),
             pltpu.VMEM((groups, groups, rank, LANES), bf16),
@@ -283,7 +318,7 @@
             dma((10,)), dma((blocks,)),
             dma((count,)), dma((count,)), dma((count,)), dma((count,)),
             dma((stages,)), dma((stages,)), dma((stages,)), dma((stages,)),
-            dma, dma, dma, dma,
+            dma, dma, dma, dma, pltpu.SemaphoreType.REGULAR,
         ],
         compiler_params=pltpu.CompilerParams(
             collective_id=0, has_side_effects=True, vmem_limit_bytes=58 * 1024 * 1024

time: 58.8 us -> 57 us (0.969)
  Pallas kernels: 55.4 us -> 53.2 us
    pallas_call x1, Pallas kernels: 55.4 us -> 53.2 us  [on_device(): pl.pallas_call(functools.partial(kernel, rows, cols, pieces), out_shape=p...]
where the time goes in v2:
time: 57 us; the launch traced here: 56.5 us
  Pallas kernels  53.2 us (93%)
  local copies, waits for them, and re-layouts  2.02 us (4%)
  between operations  1.3 us (2%)
    pallas_call x1, Pallas kernels, on_device(): pl.pallas_call(functools.partial(kernel, rows, cols, pieces), out_shape=p...  53.2 us
    unnamed x1, local copies, waits for them, and re-layouts  2.02 us

profile of v2, /device:TPU:0, one launch (start us, length us, event | category | flops | bytes accessed | tf_op | source)
XLA Modules:
  0.0 56.5 jit_solution(16258794040117975424)
XLA Ops:
  1.3 53.2 %shard_map.100 = f32[2048,512]{1,0:T(8,128)S(1)} custom-call(s32[1,1]{1,0:T(1,128)S(6)} %copy.13.near_hbm, s32[1,1]{1,0:T(1,128)S(6)} %copy.14.count_hbm, s32[1,64]{1,0:T(1,128)} %bitcast.22, s32[1,64]{1,0:T(1,128)} %bitcast.23, bf16[2048,512]{1,0:T(8,128)(2,1)} %bitcast.18, bf16[32,2048]{1,0:T(8,128)(2,1)} %bitcast.20, bf16[32,2048]{1,0:T(8,128)(2,1)} %bitcast.21, ...), custom_call_target="tpu_custom_call" | custom-call | tf_op jit(solution)/shard_map/pallas_call | solution.py:291
  54.5 2.0 %copy.12 = f32[1,1,2048,512]{3,2,1,0:T(8,128)} copy(f32[1,1,2048,512]{3,2,1,0:T(8,128)S(1)} %bitcast.15) | data formatting | bytes 8388608

commit v3 on v2

--- a/solution.py
+++ b/solution.py
@@ -12,7 +12,7 @@
 LANES = 128
 TILE = 256
 NEAR_TILE = 512
-EARLY = 10
+FINAL_STEPS = 4
 
 
 def contract(a, b):
@@ -22,19 +22,24 @@
 
 
 def pieces_of(leaf, blocks):
-    quarter = leaf // 4
-    pieces = [(c, r * quarter, quarter) for c in range(blocks) for r in range(4)]
-    c, start, size = pieces.pop()
-    return pieces + [(c, start, size // 2), (c, start + size // 2, size // 2)]
+    half, quarter, eighth = leaf // 2, leaf // 4, leaf // 8
+    pieces = [(c, 0, leaf) for c in range(blocks - 2)]
+    c = blocks - 2
+    lent = leaf // 8
+    pieces += [(c, 0, half), (c, half, half - lent), (c, leaf - lent, lent)]
+    c = blocks - 1
+    pieces += [(c, 0, half), (c, half, quarter)]
+    pieces += [(c, leaf - 2 * eighth, eighth), (c, leaf - eighth, eighth)]
+    return pieces
 
 
 def kernel(
     rows, cols, pieces,
     near_hbm, count_hbm, tgt_hbm, rank_hbm, x_hbm, rb_hbm, cb_hbm, coup_hbm, self_hbm, side_hbm,
-    out_ref,
+    out_ref, turned, ending,
     near_ref, count_ref, tgt_ref, rank_ref, xf, xc, rb_ref, cb_ref, coup_ref, self_v, side_v,
-    above, below, turned, table, flat, mbuf, dpart, dcore, mout, min_ref,
-    load_sem, xc_sem, up_s, up_r, dn_s, dn_r, c_s, c_r, m_s, m_r, d_s, d_r, e_s, e_r, relay,
+    beside, table, flat, mbuf, dpart, dcore, mout, min_ref,
+    load_sem, xc_sem, far_s, far_r, close_s, close_r, c_s, c_r, m_s, m_r, d_s, d_r, e_s, e_r, help_s, relay,
 ):
     half_chips = rows // CORES // 2
     groups = cols * half_chips
@@ -50,9 +55,9 @@
     def at_group(g):
         return (((lax.rem(g, half_chips)) * 2 + mirror) * CORES + core, g // half_chips)
 
-    after = (lax.rem(row + 1, rows), col)
-    before = (lax.rem(row + rows - 1, rows), col)
     partner = (chip * CORES + (1 - core), col)
+    away = (lax.rem(row + rows + 2 * core - 1, rows), col)
+    partners_away = (lax.rem(chip * CORES + (1 - core) + rows + 1 - 2 * core, rows), col)
     opposite = ((pair * 2 + (1 - mirror)) * CORES + core, col)
     strides = []
     while groups >> (len(strides) + 1):
@@ -63,7 +68,7 @@
     quad = lax.rem(col, 4)
     middle = lax.rem((quad + 1) // 2, 2)
     between = (row, col + 3 - 2 * quad)
-    friends = [after, before, opposite]
+    friends = [partner, away, opposite]
     friends += [d for d, h in zip(others, strides) if not (relayed and h == 2 * half_chips)]
     barrier = pltpu.get_barrier_semaphore()
     for friend in friends:
@@ -110,20 +115,28 @@
             src_ref=src, dst_ref=dst, send_sem=s, recv_sem=r, device_id=to, device_id_type=MESH
         )
 
-    hops = []
+    far, close = [], []
     for i, (c, start, size) in enumerate(pieces):
         part = pl.ds(start, size)
-        hops.append((
-            send(xc.at[c, part], above.at[c, part], up_s.at[i], up_r.at[i], after),
-            send(xc.at[c, part], below.at[c, part], dn_s.at[i], dn_r.at[i], before),
-        ))
-
-    def launch(some):
-        for up, down in some:
-            up.start()
-            down.start()
-
-    launch(hops[:EARLY])
+        far.append(
+            send(xc.at[c, part], beside.at[1 - core, c, part], far_s.at[i], far_r.at[i], away)
+        )
+        close.append(
+            send(xc.at[c, part], beside.at[core, c, part], close_s.at[i], close_r.at[i], partner)
+        )
+    early, last = blocks - 1, len(pieces) - 1
+    lent = early + 1
+    c, start, size = pieces[lent]
+    part = pl.ds(start, size)
+    helper = core == 1
+    lends = chip != rows // CORES - 1
+    relief = send(
+        beside.at[1 - core, c, part], beside.at[core, c, part], help_s, far_r.at[lent],
+        partners_away,
+    )
+
+    for copy in far[:early] + close:
+        copy.start()
     if relayed:
 
         @pl.when(middle == 1)
@@ -212,12 +225,11 @@
 
     def neighbour(c, some):
         for i in some:
-            hops[i][0].wait()
-            hops[i][1].wait()
+            far[i].wait_recv()
         part = pl.ds(pieces[some[0]][1], sum(pieces[i][2] for i in some))
         values = (
-            above[c, part, :].astype(jnp.float32) * from_above
-            + below[c, part, :].astype(jnp.float32) * from_below
+            beside[0, c, part, :].astype(jnp.float32) * from_above
+            + beside[1, c, part, :].astype(jnp.float32) * from_below
         ).astype(jnp.bfloat16)
         return part, values, pl.ds(c * LANES, LANES)
 
@@ -238,7 +250,20 @@
     mout[...] = (dpart[2 * core + 1 - mirror] + dcore[1 - mirror]).astype(jnp.bfloat16)
     cross = send(mout, min_ref, e_s, e_r, opposite)
     cross.start()
-    launch(hops[EARLY:])
+    for copy in close:
+        copy.wait()
+    for i in range(early, len(pieces)):
+        if i == lent:
+
+            @pl.when(helper & lends)
+            def _():
+                relief.start()
+
+            @pl.when(helper | jnp.logical_not(lends))
+            def _():
+                far[lent].start()
+        else:
+            far[i].start()
     for c in range(blocks - 2):
         near(c, members(c))
     cross.wait()
@@ -255,7 +280,6 @@
     lax.fori_loop(0, tiles, distant, 0)
     for c in range(blocks - 2, blocks - 1):
         near(c, members(c))
-    last = len(pieces) - 1
     final = pl.ds(pieces[last][1], pieces[last][2])
 
     def turn(m, carry):
@@ -266,12 +290,43 @@
     lax.fori_loop(0, tiles, turn, 0)
     for i in members(blocks - 1)[:-1]:
         near(blocks - 1, [i])
-    _, values, lanes = neighbour(blocks - 1, [last])
-    for m in range(leaf // NEAR_TILE):
-        at = pl.ds(m * NEAR_TILE, NEAR_TILE)
-        out_ref[at, lanes] += jnp.dot(
-            turned[at, :], values, preferred_element_type=jnp.float32
-        )
+    _, values, _ = neighbour(blocks - 1, [last])
+    ending[...] = values
+    for i, copy in enumerate(far):
+        if i != lent:
+            copy.wait_send()
+
+    @pl.when(helper & lends)
+    def _():
+        relief.wait_send()
+
+    @pl.when(helper | jnp.logical_not(lends))
+    def _():
+        far[lent].wait_send()
+
+
+def finish(acc_ref, turned_ref, ending_ref, out_ref, block, body_sem, block_sem):
+    leaf, width = acc_ref.shape
+    body = width - LANES
+    step = leaf // FINAL_STEPS
+    copies = []
+    for m in range(FINAL_STEPS):
+        at = pl.ds(m * step, step)
+        copies.append(pltpu.make_async_copy(
+            acc_ref.at[at, pl.ds(0, body)], out_ref.at[at, pl.ds(0, body)], body_sem.at[m]
+        ))
+        copies[-1].start()
+    for m in range(FINAL_STEPS):
+        at = pl.ds(m * step, step)
+        block[at, :] = acc_ref[at, pl.ds(body, LANES)] + jnp.dot(
+            turned_ref[at, :], ending_ref[...], preferred_element_type=jnp.float32
+        )
+        copies.append(pltpu.make_async_copy(
+            block.at[at], out_ref.at[at, pl.ds(body, LANES)], block_sem.at[m]
+        ))
+        copies[-1].start()
+    for copy in copies:
+        copy.wait()
 
 
 def on_device(
@@ -288,11 +343,17 @@
     hbm = pl.BlockSpec(memory_space=pltpu.HBM)
     dma = pltpu.SemaphoreType.DMA
     bf16 = jnp.bfloat16
-    gradient = pl.pallas_call(
+    vmem = pl.BlockSpec(memory_space=pltpu.VMEM)
+    final = pieces[-1][2]
+    acc, turned, ending = pl.pallas_call(
         functools.partial(kernel, rows, cols, pieces),
-        out_shape=pltpu.VMEM((leaf, width), jnp.float32),
+        out_shape=(
+            pltpu.VMEM((leaf, width), jnp.float32),
+            pltpu.VMEM((leaf, final), bf16),
+            pltpu.VMEM((final, LANES), bf16),
+        ),
         in_specs=[hbm] * 10,
-        out_specs=pl.BlockSpec(memory_space=pltpu.VMEM),
+        out_specs=(vmem, vmem, vmem),
         scratch_shapes=[
             pltpu.VMEM((1, 1), jnp.int32),
             pltpu.VMEM((1, 1), jnp.int32),
@@ -305,9 +366,7 @@
             pltpu.VMEM((rank * rank, slots), bf16),
             pltpu.VMEM((leaf, leaf), bf16),
             pltpu.VMEM((leaf, leaf), bf16),
-            pltpu.VMEM((blocks, leaf, LANES), bf16),
-            pltpu.VMEM((blocks, leaf, LANES), bf16),
-            pltpu.VMEM((leaf, pieces[-1][2]), bf16),
+            pltpu.VMEM((2, blocks, leaf, LANES), bf16),
             pltpu.VMEM((groups, rank, width), bf16),
             pltpu.VMEM((rank, groups, LANES), jnp.float32),
             pltpu.VMEM((groups, groups, rank, LANES), bf16),
@@ -318,16 +377,26 @@
             dma((10,)), dma((blocks,)),
             dma((count,)), dma((count,)), dma((count,)), dma((count,)),
             dma((stages,)), dma((stages,)), dma((stages,)), dma((stages,)),
-            dma, dma, dma, dma, pltpu.SemaphoreType.REGULAR,
+            dma, dma, dma, dma, dma, pltpu.SemaphoreType.REGULAR,
         ],
         compiler_params=pltpu.CompilerParams(
-            collective_id=0, has_side_effects=True, vmem_limit_bytes=58 * 1024 * 1024
+            collective_id=0, has_side_effects=True, vmem_limit_bytes=54 * 1024 * 1024
         ),
     )(
         near_side, adm_count, adm_targets.reshape(1, slots), adm_ranks.reshape(1, slots),
         residual[0, 0], row_cluster_basis[0, 0].T, column_cluster_basis[0, 0].T,
         couplings.reshape(slots, rank * rank).T, self_tiles[0, 0], side_tiles[0, 0],
     )
+    gradient = pl.pallas_call(
+        finish,
+        out_shape=jax.ShapeDtypeStruct((leaf, width), jnp.float32),
+        in_specs=[vmem] * 3,
+        out_specs=pl.BlockSpec(memory_space=pl.ANY),
+        scratch_shapes=[
+            pltpu.VMEM((leaf, LANES), jnp.float32), dma((FINAL_STEPS,)), dma((FINAL_STEPS,)),
+        ],
+        compiler_params=pltpu.CompilerParams(vmem_limit_bytes=16 * 1024 * 1024),
+    )(acc, turned, ending)
     return gradient[None, None]
 
 

time: 57 us -> 56.1 us (0.984)
  local copies, waits for them, and re-layouts: 2.02 us -> 0 us
  Pallas kernels: 53.2 us -> 54.6 us
    unnamed x1 -> x0, local copies, waits for them, and re-layouts: 2.02 us -> none
    pallas_call x1 -> x2, Pallas kernels: 53.2 us -> 54.6 us  [the longest x1 52.5 us: on_device(): pl.pallas_call(functools.partial(kernel, rows, cols, pieces), out_shape=(...]
where the time goes in v3:
time: 56.1 us; the launch traced here: 55.9 us
  Pallas kernels  54.6 us (97%)
  between operations  1.3 us (2%)
    pallas_call x1, Pallas kernels, on_device(): pl.pallas_call(functools.partial(kernel, rows, cols, pieces), out_shape=(...  52.5 us
    pallas_call x1, Pallas kernels, on_device(): pl.pallas_call(finish, out_shape=jax.ShapeDtypeStruct((leaf, width), jnp....  2.08 us

profile of v3, /device:TPU:0, one launch (start us, length us, event | category | flops | bytes accessed | tf_op | source)
XLA Modules:
  0.0 55.9 jit_solution(12588250644359575604)
XLA Ops:
  1.3 52.5 %shard_map.100 = (f32[2048,512]{1,0:T(8,128)S(1)}, bf16[2048,256]{1,0:T(8,128)(2,1)S(1)}, bf16[256,128]{1,0:T(8,128)(2,1)S(1)}) custom-call(s32[1,1]{1,0:T(1,128)S(6)} %copy.11.near_hbm, s32[1,1]{1,0:T(1,128)S(6)} %copy.12.count_hbm, s32[1,64]{1,0:T(1,128)} %bitcast.21, s32[1,64]{1,0:T(1,128)} %bitcast.22, bf16[2048,512]{1,0:T(8,128)(2,1)} %bitcast.17, ...), custom_call_target="tpu_custom_call" | custom-call | tf_op jit(solution)/shard_map/pallas_call | solution.py:348
  53.8 2.1 %shard_map.101 = f32[2048,512]{1,0:T(8,128)} custom-call(f32[2048,512]{1,0:T(8,128)S(1)} %get-tuple-element.8.acc_ref, bf16[2048,256]{1,0:T(8,128)(2,1)S(1)} %get-tuple-element.9.turned_ref, bf16[256,128]{1,0:T(8,128)(2,1)S(1)} %get-tuple-element.10.ending_ref), custom_call_target="tpu_custom_call" | custom-call | tf_op jit(solution)/shard_map/pallas_call | solution.py:390

commit v4 on v3

--- a/solution.py
+++ b/solution.py
@@ -22,14 +22,13 @@
 
 
 def pieces_of(leaf, blocks):
-    half, quarter, eighth = leaf // 2, leaf // 4, leaf // 8
+    half, quarter = leaf // 2, leaf // 4
     pieces = [(c, 0, leaf) for c in range(blocks - 2)]
     c = blocks - 2
-    lent = leaf // 8
+    lent = leaf // 16
     pieces += [(c, 0, half), (c, half, half - lent), (c, leaf - lent, lent)]
     c = blocks - 1
-    pieces += [(c, 0, half), (c, half, quarter)]
-    pieces += [(c, leaf - 2 * eighth, eighth), (c, leaf - eighth, eighth)]
+    pieces += [(c, 0, half), (c, half, quarter), (c, leaf - quarter, quarter)]
     return pieces
 
 
@@ -124,12 +123,11 @@
         close.append(
             send(xc.at[c, part], beside.at[core, c, part], close_s.at[i], close_r.at[i], partner)
         )
-    early, last = blocks - 1, len(pieces) - 1
+    early = blocks - 1
     lent = early + 1
     c, start, size = pieces[lent]
     part = pl.ds(start, size)
-    helper = core == 1
-    lends = chip != rows // CORES - 1
+    helper = core == jnp.where(chip == rows // CORES - 1, 0, 1)
     relief = send(
         beside.at[1 - core, c, part], beside.at[core, c, part], help_s, far_r.at[lent],
         partners_away,
@@ -255,12 +253,9 @@
     for i in range(early, len(pieces)):
         if i == lent:
 
-            @pl.when(helper & lends)
+            @pl.when(helper)
             def _():
                 relief.start()
-
-            @pl.when(helper | jnp.logical_not(lends))
-            def _():
                 far[lent].start()
         else:
             far[i].start()
@@ -280,7 +275,9 @@
     lax.fori_loop(0, tiles, distant, 0)
     for c in range(blocks - 2, blocks - 1):
         near(c, members(c))
-    final = pl.ds(pieces[last][1], pieces[last][2])
+    closing = members(blocks - 1)[-1:]
+    rows_left = sum(pieces[i][2] for i in closing)
+    final = pl.ds(leaf - rows_left, rows_left)
 
     def turn(m, carry):
         at = pl.ds(pl.multiple_of(m * TILE, TILE), TILE)
@@ -290,18 +287,15 @@
     lax.fori_loop(0, tiles, turn, 0)
     for i in members(blocks - 1)[:-1]:
         near(blocks - 1, [i])
-    _, values, _ = neighbour(blocks - 1, [last])
+    _, values, _ = neighbour(blocks - 1, closing)
     ending[...] = values
     for i, copy in enumerate(far):
         if i != lent:
             copy.wait_send()
 
-    @pl.when(helper & lends)
+    @pl.when(helper)
     def _():
         relief.wait_send()
-
-    @pl.when(helper | jnp.logical_not(lends))
-    def _():
         far[lent].wait_send()
 
 
@@ -344,7 +338,7 @@
     dma = pltpu.SemaphoreType.DMA
     bf16 = jnp.bfloat16
     vmem = pl.BlockSpec(memory_space=pltpu.VMEM)
-    final = pieces[-1][2]
+    final = sum(p[2] for p in pieces[-1:])
     acc, turned, ending = pl.pallas_call(
         functools.partial(kernel, rows, cols, pieces),
         out_shape=(

time: 56.1 us -> 55.3 us (0.986)
  Pallas kernels: 54.6 us -> 53.9 us
    pallas_call x1, Pallas kernels: 52.5 us -> 51.8 us  [on_device(): pl.pallas_call(functools.partial(kernel, rows, cols, pieces), out_shape=(...]
where the time goes in v4:
time: 55.3 us; the launch traced here: 55.2 us
  Pallas kernels  53.9 us (97%)
  between operations  1.3 us (2%)
    pallas_call x1, Pallas kernels, on_device(): pl.pallas_call(functools.partial(kernel, rows, cols, pieces), out_shape=(...  51.8 us
    pallas_call x1, Pallas kernels, on_device(): pl.pallas_call(finish, out_shape=jax.ShapeDtypeStruct((leaf, width), jnp....  2.08 us

profile of v4, /device:TPU:0, one launch (start us, length us, event | category | flops | bytes accessed | tf_op | source)
XLA Modules:
  0.0 55.2 jit_solution(15983720343115951976)
XLA Ops:
  1.3 51.8 %shard_map.100 = (f32[2048,512]{1,0:T(8,128)S(1)}, bf16[2048,512]{1,0:T(8,128)(2,1)S(1)}, bf16[512,128]{1,0:T(8,128)(2,1)S(1)}) custom-call(s32[1,1]{1,0:T(1,128)S(6)} %copy.11.near_hbm, s32[1,1]{1,0:T(1,128)S(6)} %copy.12.count_hbm, s32[1,64]{1,0:T(1,128)} %bitcast.21, s32[1,64]{1,0:T(1,128)} %bitcast.22, bf16[2048,512]{1,0:T(8,128)(2,1)} %bitcast.17, ...), custom_call_target="tpu_custom_call" | custom-call | tf_op jit(solution)/shard_map/pallas_call | solution.py:342
  53.1 2.1 %shard_map.101 = f32[2048,512]{1,0:T(8,128)} custom-call(f32[2048,512]{1,0:T(8,128)S(1)} %get-tuple-element.8.acc_ref, bf16[2048,512]{1,0:T(8,128)(2,1)S(1)} %get-tuple-element.9.turned_ref, bf16[512,128]{1,0:T(8,128)(2,1)S(1)} %get-tuple-element.10.ending_ref), custom_call_target="tpu_custom_call" | custom-call | tf_op jit(solution)/shard_map/pallas_call | solution.py:384

commit v5 on v4

--- a/solution.py
+++ b/solution.py
@@ -25,7 +25,7 @@
     half, quarter = leaf // 2, leaf // 4
     pieces = [(c, 0, leaf) for c in range(blocks - 2)]
     c = blocks - 2
-    lent = leaf // 16
+    lent = leaf // 8 - leaf // 32
     pieces += [(c, 0, half), (c, half, half - lent), (c, leaf - lent, lent)]
     c = blocks - 1
     pieces += [(c, 0, half), (c, half, quarter), (c, leaf - quarter, quarter)]

time: 55.3 us -> 55.1 us (level)
  no operation moved by 1% of the time
where the time goes in v5:
time: 55.1 us; the launch traced here: 54.8 us
  Pallas kernels  53.5 us (97%)
  between operations  1.3 us (2%)
    pallas_call x1, Pallas kernels, on_device(): pl.pallas_call(functools.partial(kernel, rows, cols, pieces), out_shape=(...  51.5 us
    pallas_call x1, Pallas kernels, on_device(): pl.pallas_call(finish, out_shape=jax.ShapeDtypeStruct((leaf, width), jnp....  2.08 us

profile of v5, /device:TPU:0, one launch (start us, length us, event | category | flops | bytes accessed | tf_op | source)
XLA Modules:
  0.0 54.8 jit_solution(14013400567176917119)
XLA Ops:
  1.3 51.5 %shard_map.100 = (f32[2048,512]{1,0:T(8,128)S(1)}, bf16[2048,512]{1,0:T(8,128)(2,1)S(1)}, bf16[512,128]{1,0:T(8,128)(2,1)S(1)}) custom-call(s32[1,1]{1,0:T(1,128)S(6)} %copy.11.near_hbm, s32[1,1]{1,0:T(1,128)S(6)} %copy.12.count_hbm, s32[1,64]{1,0:T(1,128)} %bitcast.21, s32[1,64]{1,0:T(1,128)} %bitcast.22, bf16[2048,512]{1,0:T(8,128)(2,1)} %bitcast.17, ...), custom_call_target="tpu_custom_call" | custom-call | tf_op jit(solution)/shard_map/pallas_call | solution.py:342
  52.8 2.1 %shard_map.101 = f32[2048,512]{1,0:T(8,128)} custom-call(f32[2048,512]{1,0:T(8,128)S(1)} %get-tuple-element.8.acc_ref, bf16[2048,512]{1,0:T(8,128)(2,1)S(1)} %get-tuple-element.9.turned_ref, bf16[512,128]{1,0:T(8,128)(2,1)S(1)} %get-tuple-element.10.ending_ref), custom_call_target="tpu_custom_call" | custom-call | tf_op jit(solution)/shard_map/pallas_call | solution.py:384
